TPU v7x, 32 devices: a whole 2x2x4 slice. The times are simulated.
32 devices in a mesh: replica: 2 (over core), fsdp: 16 (over z, y, x).
Axes of the slice: x: 2, y: 2, z: 4, core: 2. Of those that a mesh axis runs over, the one named last changes fastest.
Arguments:
- activations: bfloat16 [16384, 4096], P(('replica', 'fsdp')), may hold values from -6 to 6
- queries: bfloat16 [16384, 2048], P(('replica', 'fsdp')), may hold values from -60 to 60
- out_grad: bfloat16 [16384, 2048], P(('replica', 'fsdp')), may hold values from -6 to 6
- lengths: int32 [64], P(('replica', 'fsdp')), may hold values from 32 to 256
- norm_gain: float32 [4096], replicated, may hold values from 0.5 to 7
- key_master: float32 [4096, 512], P('fsdp'), may hold values from -0.09375 to 0.09375
- value_master: float32 [4096, 512], P('fsdp'), may hold values from -0.09375 to 0.09375
Outputs:
- key_direction: float32 [4096, 512], P('fsdp')
- value_direction: float32 [4096, 512], P('fsdp')
All inputs are finite; a program needn't handle non-finite values.
Results may differ from a plain program's by a relative error of at most 0.009.
The roundings to bfloat16 on the way count: a program that leaves them out, or rounds other values in their place, can miss the bound.
Values may be sent and summed in bfloat16 or wider, within the bound.
A program may use at most 128 MiB of HBM per device.

v0:
```python
import jax
import jax.numpy as jnp
from jax import lax
from jax.sharding import PartitionSpec as P

D = 4096
HD = 128
KVH = 4
GROUP = 4
LEN = 256


def attend(query_seq, key_seq, value_seq, grad_seq, length):
    scale_factor = 1.0 / HD**0.5
    positions = jnp.arange(LEN, dtype=jnp.int32)
    allowed = (positions[None, :] <= positions[:, None]) & (positions[None, :] < length)
    query_float = query_seq.astype(jnp.float32).reshape(LEN, KVH, GROUP, HD)
    key_float = key_seq.astype(jnp.float32).reshape(LEN, KVH, HD)
    value_float = value_seq.astype(jnp.float32).reshape(LEN, KVH, HD)
    scores = jnp.einsum("qhgd,khd->hgqk", query_float, key_float) * scale_factor
    scores = jnp.where(allowed[None, None], scores, jnp.float32(-1e30))
    row_peak = jnp.max(scores, axis=-1, keepdims=True)
    exponent = jnp.exp(scores - row_peak)
    probs = exponent / jnp.sum(exponent, axis=-1, keepdims=True)
    probs_low = lax.optimization_barrier(probs.astype(jnp.bfloat16))
    probs_back = probs_low.astype(jnp.float32)
    attended = jnp.einsum("hgqk,khd->qhgd", probs_back, value_float).astype(jnp.bfloat16)
    attended = lax.optimization_barrier(attended).astype(jnp.float32)
    live_rows = (positions < length).astype(jnp.float32)
    grad_float = (
        grad_seq.astype(jnp.float32).reshape(LEN, KVH, GROUP, HD) * live_rows[:, None, None, None]
    )
    row_delta = jnp.transpose(jnp.sum(grad_float * attended, axis=-1), (1, 2, 0))[..., None]
    value_grad = jnp.einsum("hgqk,qhgd->khd", probs_back, grad_float).astype(jnp.bfloat16)
    prob_grad = jnp.einsum("qhgd,khd->hgqk", grad_float, value_float)
    score_grad = lax.optimization_barrier((probs * (prob_grad - row_delta)).astype(jnp.bfloat16))
    key_grad = (
        jnp.einsum("hgqk,qhgd->khd", score_grad.astype(jnp.float32), query_float) * scale_factor
    ).astype(jnp.bfloat16)
    return (key_grad.reshape(LEN, KVH * HD), value_grad.reshape(LEN, KVH * HD))


def transposed_product(columns, combined):
    return lax.dot_general(
        columns, combined, (((0,), (0,)), ((), ())), preferred_element_type=jnp.float32
    )


def local(activations, queries, out_grad, lengths, norm_gain, key_master, value_master):
    tok_rows = activations.shape[0]
    width = key_master.shape[1]
    shard_rows = key_master.shape[0]
    act_float = activations.astype(jnp.float32)
    inverse = lax.rsqrt(jnp.mean(act_float * act_float, axis=-1, keepdims=True) + 1e-05)
    normed = (act_float * inverse * norm_gain[None, :]).astype(jnp.bfloat16)
    columns = normed
    key_sum = jnp.dot(
        columns,
        lax.all_gather(key_master.astype(jnp.bfloat16), "fsdp", axis=0, tiled=True),
        preferred_element_type=jnp.float32,
    )
    value_sum = jnp.dot(
        columns,
        lax.all_gather(value_master.astype(jnp.bfloat16), "fsdp", axis=0, tiled=True),
        preferred_element_type=jnp.float32,
    )
    key_proj = key_sum.astype(jnp.bfloat16)
    value_proj = value_sum.astype(jnp.bfloat16)
    seq_count = lengths.shape[0]
    qwidth = queries.shape[1]

    def one_seq(packed):
        return attend(packed[0], packed[1], packed[2], packed[3], packed[4])

    key_grad, value_grad = lax.map(
        one_seq,
        (
            queries.reshape(seq_count, LEN, qwidth),
            key_proj.reshape(seq_count, LEN, width),
            value_proj.reshape(seq_count, LEN, width),
            out_grad.reshape(seq_count, LEN, qwidth),
            lengths,
        ),
    )
    combined = jnp.concatenate(
        [key_grad.reshape(tok_rows, width), value_grad.reshape(tok_rows, width)], axis=1
    )
    replicas = lax.axis_size("replica")
    shards = lax.axis_size("fsdp")
    piece_rows = shard_rows // replicas
    permuted = (
        normed.reshape(tok_rows, shards, replicas, piece_rows)
        .transpose(0, 2, 1, 3)
        .reshape(tok_rows, shards * shard_rows)
    )
    columns = permuted
    owned_grad = lax.psum_scatter(
        transposed_product(columns, combined), ("replica", "fsdp"), scatter_dimension=0, tiled=True
    )
    total_sq = lax.psum(jnp.sum(owned_grad * owned_grad), ("replica", "fsdp"))
    summed = lax.all_gather(owned_grad.astype(jnp.bfloat16), "replica", axis=0, tiled=True).astype(
        owned_grad.dtype
    )
    unit_scale = jnp.sqrt(jnp.float32(2 * D * width)) / jnp.sqrt(total_sq + 1e-06)
    return (unit_scale * summed[:, :width], unit_scale * summed[:, width:])


def solution(mesh):
    in_specs = (
        P(("replica", "fsdp"), None),
        P(("replica", "fsdp"), None),
        P(("replica", "fsdp"), None),
        P(("replica", "fsdp")),
        P(),
        P("fsdp", None),
        P("fsdp", None),
    )
    out_specs = (P("fsdp", None), P("fsdp", None))
    return jax.shard_map(local, mesh=mesh, in_specs=in_specs, out_specs=out_specs, check_vma=False)
```

profile of v0, /device:TPU:7, one launch (start us, length us, event | category | flops | bytes accessed | tf_op | source)
XLA Modules:
  0.0 638.2 jit_solution(8576653580051986996)
XLA Ops:
  7.2 1.8 convert_element_type.74
  9.1 1.8 convert_element_type.72
  11.0 6.5 %copy.41 = bf16[512,4096]{0,1:T(8,128)(2,1)} copy(bf16[512,4096]{1,0:T(8,128)(2,1)} %param.9) | data formatting | bytes 8388608 | tf_op args[0]
  17.4 3.3 fusion.24
  21.0 1.1 fusion.26
  22.1 1.9 copy-done.2
  24.0 2.4 copy.42
  26.4 58.6 %all-gather.5.cloned.1.call-done = bf16[4096,512]{1,0:T(8,128)(2,1)} async-done(((bf16[256,512]{1,0:T(8,128)(2,1)}), bf16[4096,512]{1,0:T(8,128)(2,1)}) %all-gather.5.cloned.1.call-update) | async-done | bytes 4194320 | tf_op jit(solution)/shard_map/all_gather | solution.py:64
  85.0 5.8 convolution_convert_fusion.1
  90.8 71.2 %all-gather.3.cloned.1.call-done = bf16[4096,512]{1,0:T(8,128)(2,1)} async-done(((bf16[256,512]{1,0:T(8,128)(2,1)}), bf16[4096,512]{1,0:T(8,128)(2,1)}) %all-gather.3.cloned.1.call-update) | async-done | bytes 4194320 | tf_op jit(solution)/shard_map/all_gather | solution.py:59
  162.0 6.6 %convolution_convert_fusion.2 = bf16[512,512]{1,0:T(8,128)(2,1)} fusion(bf16[512,4096]{0,1:T(8,128)(2,1)} %copy-done.2, bf16[4096,512]{1,0:T(8,128)(2,1)} %all-gather.3.cloned.1.call-done), kind=kOutput, calls=%fused_computation.44 | convolution fusion | flops 2147745792 | bytes 8912896 | tf_op jit(solution)/shard_map/dot_general | solution.py:57
  168.6 41.5 %while.12 = (s32[]{:T(128)}, bf16[2,256,512]{2,1,0:T(8,128)(2,1)}, bf16[2,256,512]{2,1,0:T(8,128)(2,1)}, bf16[2,256,2048]{2,1,0:T(8,128)(2,1)}, s32[2]{0:T(128)S...) while((s32[]{:T(128)}, bf16[2,256,512]{2,1,0:T(8,128)(2,1)}, ...), condition=%wide.region_5.6_spmd, body=%wide.region_1.5_spmd.sunk | while | flops 1358427136 | bytes 69686040 | solution.py:75
  171.1 1.0 constant_dynamic-slice_fusion.8
  172.0 0.8 copy.77
  172.9 1.3 constant_dynamic-slice_fusion.10
  174.7 1.3 constant_dynamic-slice_fusion.9
  176.5 4.4 fusion.74
  181.0 2.6 fusion.75
  185.8 0.9 fusion.80
  191.8 1.0 constant_dynamic-slice_fusion.8
  192.8 0.8 copy.77
  193.7 1.3 constant_dynamic-slice_fusion.10
  195.5 1.3 constant_dynamic-slice_fusion.9
  197.3 4.4 fusion.74
  201.7 2.6 fusion.75
  206.5 0.9 fusion.80
  210.1 12.7 %fusion.27 = f32[4096,1024]{1,0:T(8,128)} fusion(bf16[512,4096]{0,1:T(8,128)(2,1)} %bitcast.135, bf16[512,512]{1,0:T(8,128)(2,1)} %bitcast.138, bf16[512,512]{1,0:T(8,128)(2,1)} %bitcast.139), kind=kOutput, calls=%fused_computation.45 | convolution fusion | flops 4297064448 | bytes 22020096 | tf_op jit(solution)/shard_map/dot_general | solution.py:44
  222.9 355.9 %reduce-scatter.2.cloned.1.call-done = f32[128,1024]{1,0:T(8,128)} async-done(((f32[4096,1024]{1,0:T(8,128)}), f32[128,1024]{1,0:T(8,128)}) %reduce-scatter.2.cloned.1.call-update) | async-done | bytes 524304 | tf_op jit(solution)/shard_map/reduce_scatter | solution.py:97
  578.8 2.0 multiply_reduce_fusion
  580.7 44.4 %psum.7 = f32[]{:T(128)} all-reduce(f32[]{:T(128)} %get-tuple-element.93), channel_id=1, replica_groups=mesh['replica'=2,'fsdp'=16] {'replica','fsdp'}, use_global_device_ids=true, to_apply=%region_8.9 | all-reduce | flops 1 | bytes 8 | tf_op jit(solution)/shard_map/psum | solution.py:100
  625.8 4.7 all_gather.11
  630.6 1.1 slice_multiply_fusion
  (67 shorter events, 17.1 us)
Async XLA Ops:
  7.2 77.8 %all-gather.5.cloned.1.call-start = ((), (), s32[]{:S(2)}) async-start(), calls=%async_computation.2 | async-start | bytes 4456448 | tf_op jit(solution)/shard_map/all_gather | solution.py:64
  9.0 153.0 %all-gather.3.cloned.1.call-start = ((), (), s32[]{:S(2)}) async-start(), calls=%async_computation.1 | async-start | bytes 4456448 | tf_op jit(solution)/shard_map/all_gather | solution.py:59
  10.9 567.9 %reduce-scatter.2.cloned.1.call-start = ((), (), s32[]{:S(2)}) async-start(), calls=%async_computation.3 | async-start | bytes 17301504 | tf_op jit(solution)/shard_map/reduce_scatter | solution.py:97
  10.9 9.8 %copy-start.5 = (f32[4096]{0:T(1024)S(1)}, f32[4096]{0:T(1024)}, u32[]{:S(2)}) copy-start(f32[4096]{0:T(1024)} %param.13) | copy-start | bytes 49156
  17.4 3.5 copy-start.1
  22.1 2.0 copy-start.2
  90.8 77.8 %copy-start.8 = (s32[2]{0:T(128)S(1)}, s32[2]{0:T(128)}, u32[]{:S(2)}) copy-start(s32[2]{0:T(128)} %param.12) | copy-start | bytes 28
  168.6 4.3 copy-start.3
  183.6 2.2 copy-start
  186.7 1.1 copy-start.6
  186.7 2.7 copy-start.4
  188.6 0.8 copy-start.7
  189.4 4.3 copy-start.3
  204.3 2.2 copy-start
  207.4 1.1 copy-start.6
  207.5 2.7 copy-start.4
  209.3 0.8 copy-start.7
Sparse Core Ops, SparseCore 0:
  10.7 74.2 all-gather.4
  87.8 74.1 all-gather.2
  223.0 355.6 reduce-scatter.1
where the time goes:
time: 639 us; the launch traced here: 638 us
  waiting for transfers between devices  486 us (76%)
  blocking collectives  49.1 us (8%)
  matrix products  39.9 us (6%)
  local copies, waits for them, and re-layouts  28.6 us (4%)
  other arithmetic  20 us (3%)
  between operations  14.5 us (2%)
    reduce_scatter x1, waiting for transfers between devices, local(): lax.psum_scatter(transposed_product(columns, combined), ('replica', 'fsdp...  356 us
    all_gather x1, waiting for transfers between devices, local(): lax.all_gather(key_master.astype(jnp.bfloat16), 'fsdp', axis=0, tiled=True)  71.2 us
    all_gather x1, waiting for transfers between devices, local(): lax.all_gather(value_master.astype(jnp.bfloat16), 'fsdp', axis=0, tiled=T...  58.6 us
    psum x1, blocking collectives, local(): total_sq = lax.psum(jnp.sum(owned_grad * owned_grad), ('replica', 'fsdp'))  44.4 us
    dynamic_slice x18, local copies, waits for them, and re-layouts, local(): lax.map(one_seq, (queries.reshape(seq_count, LEN, qwidth), key_proj.resha...  12.8 us
  transfers between devices with their start and end apart: 3, of which 3 were waited for; matrix products, arithmetic and copies ran while one was open for 3% of the time, Pallas kernels for 0%

commit v1 on v0

--- a/solution.py
+++ b/solution.py
@@ -56,7 +56,12 @@
     columns = normed
     key_sum = jnp.dot(
         columns,
-        lax.all_gather(key_master.astype(jnp.bfloat16), "fsdp", axis=0, tiled=True),
+        jnp.concatenate(
+            lax.all_to_all(
+                jnp.stack([key_master.astype(jnp.bfloat16)] * lax.axis_size("fsdp")), "fsdp", 0, 0
+            ),
+            axis=0,
+        ),
         preferred_element_type=jnp.float32,
     )
     value_sum = jnp.dot(

time: 639 us -> 633 us (level)
  waiting for transfers between devices: 486 us -> 472 us
  starting transfers between devices: 0.12 us -> 6.9 us
    all_to_all x0 -> x1, waiting for transfers between devices: none -> 83 us  [local(): lax.all_to_all(jnp.stack([key_master.astype(jnp.bfloat16)] * lax.axis_siz...]
    all_gather x1 -> x0, waiting for transfers between devices: 71.2 us -> none  [local(): lax.all_gather(key_master.astype(jnp.bfloat16), 'fsdp', axis=0, tiled=True)]
    all_gather x1, waiting for transfers between devices: 58.6 us -> 29 us  [local(): lax.all_gather(value_master.astype(jnp.bfloat16), 'fsdp', axis=0, tiled=T...]
    all_to_all x0 -> x1, starting transfers between devices: none -> 6.82 us  [local(): lax.all_to_all(jnp.stack([key_master.astype(jnp.bfloat16)] * lax.axis_siz...]
where the time goes in v1:
time: 633 us; the launch traced here: 632 us
  waiting for transfers between devices  472 us (75%)
  blocking collectives  49 us (8%)
  matrix products  40.2 us (6%)
  local copies, waits for them, and re-layouts  30.7 us (5%)
  other arithmetic  18.2 us (3%)
  between operations  14.8 us (2%)
  starting transfers between devices  6.9 us (1%)
    reduce_scatter x1, waiting for transfers between devices, local(): lax.psum_scatter(transposed_product(columns, combined), ('replica', 'fsdp...  360 us
    all_to_all x1, waiting for transfers between devices, local(): lax.all_to_all(jnp.stack([key_master.astype(jnp.bfloat16)] * lax.axis_siz...  83 us
    psum x1, blocking collectives, local(): total_sq = lax.psum(jnp.sum(owned_grad * owned_grad), ('replica', 'fsdp'))  44.3 us
    all_gather x1, waiting for transfers between devices, local(): lax.all_gather(value_master.astype(jnp.bfloat16), 'fsdp', axis=0, tiled=T...  29 us
    dot_general x1, matrix products, transposed_product(): lax.dot_general(columns, combined, (((0,), (0,)), ((), ())), preferred_el...  12.7 us
    dynamic_slice x18, local copies, waits for them, and re-layouts, local(): lax.map(one_seq, (queries.reshape(seq_count, LEN, qwidth), key_proj.resha...  12.7 us
  transfers between devices with their start and end apart: 3, of which 3 were waited for; matrix products, arithmetic and copies ran while one was open for 3% of the time, Pallas kernels for 0%

profile of v1, /device:TPU:7, one launch (start us, length us, event | category | flops | bytes accessed | tf_op | source)
XLA Modules:
  0.0 632.2 jit_solution(5360323428074929799)
XLA Ops:
  7.2 1.1 convert_element_type.72
  8.2 2.4 stack.2
  10.6 6.8 %all-to-all-start = ((bf16[16,256,512]{2,1,0:T(8,128)(2,1)}), bf16[16,256,512]{2,1,0:T(8,128)(2,1)}, u32[]{:S(2)}, u32[]{:S(2)}) async-start(bf16[16,256,512]{2,1,0:T(8,128)(2,1)} %stack.2), calls=%async_computation | async-start | bytes 8388608 | tf_op jit(solution)/shard_map/all_to_all | solution.py:60
  18.3 6.5 %copy.41 = bf16[512,4096]{0,1:T(8,128)(2,1)} copy(bf16[512,4096]{1,0:T(8,128)(2,1)} %param.9) | data formatting | bytes 8388608 | tf_op args[0]
  24.8 3.3 fusion.24
  28.3 1.1 fusion.26
  29.4 1.9 copy-done.2
  31.3 2.4 copy.42
  33.7 83.0 %all-to-all-done = bf16[16,256,512]{2,1,0:T(8,128)(2,1)} async-done(((bf16[16,256,512]{2,1,0:T(8,128)(2,1)}), bf16[16,256,512]{2,1,0:T(8,128)(2,1)}, u32[]{:S(2)}, u32[]{:S(2)}) %all-to-all-start) | async-done | bytes 4194336 | tf_op jit(solution)/shard_map/all_to_all | solution.py:60
  116.7 6.1 convolution_convert_fusion.2
  122.9 29.0 %all-gather.2.cloned.1.call-done = bf16[4096,512]{1,0:T(8,128)(2,1)} async-done(((bf16[256,512]{1,0:T(8,128)(2,1)}), bf16[4096,512]{1,0:T(8,128)(2,1)}) %all-gather.2.cloned.1.call-update) | async-done | bytes 4194320 | tf_op jit(solution)/shard_map/all_gather | solution.py:69
  151.9 6.6 %convolution_convert_fusion.1 = bf16[512,512]{1,0:T(8,128)(2,1)} fusion(bf16[512,4096]{0,1:T(8,128)(2,1)} %copy-done.2, bf16[4096,512]{1,0:T(8,128)(2,1)} %all-gather.2.cloned.1.call-done), kind=kOutput, calls=%fused_computation.43 | convolution fusion | flops 2147745792 | bytes 8912896 | tf_op jit(solution)/shard_map/dot_general | solution.py:67
  158.5 41.4 %while.12 = (s32[]{:T(128)}, bf16[2,256,512]{2,1,0:T(8,128)(2,1)}, bf16[2,256,512]{2,1,0:T(8,128)(2,1)}, bf16[2,256,2048]{2,1,0:T(8,128)(2,1)}, s32[2]{0:T(128)S...) while((s32[]{:T(128)}, bf16[2,256,512]{2,1,0:T(8,128)(2,1)}, ...), condition=%wide.region_5.6_spmd, body=%wide.region_1.5_spmd.sunk | while | flops 1358427136 | bytes 69686040 | solution.py:80
  160.7 1.0 constant_dynamic-slice_fusion.11
  161.9 0.8 copy.77
  162.7 1.3 constant_dynamic-slice_fusion.10
  164.6 1.3 constant_dynamic-slice_fusion.9
  166.4 4.4 fusion.74
  170.8 2.6 fusion.75
  175.6 0.9 fusion.80
  181.4 1.0 constant_dynamic-slice_fusion.11
  183.4 1.3 constant_dynamic-slice_fusion.10
  185.2 1.3 constant_dynamic-slice_fusion.9
  187.1 4.4 fusion.74
  191.5 2.6 fusion.75
  196.3 0.9 fusion.80
  199.9 12.7 %fusion.27 = f32[4096,1024]{1,0:T(8,128)} fusion(bf16[512,4096]{0,1:T(8,128)(2,1)} %bitcast.136, bf16[512,512]{1,0:T(8,128)(2,1)} %bitcast.139, bf16[512,512]{1,0:T(8,128)(2,1)} %bitcast.140), kind=kOutput, calls=%fused_computation.45 | convolution fusion | flops 4297064448 | bytes 22020096 | tf_op jit(solution)/shard_map/dot_general | solution.py:44
  212.6 359.8 %reduce-scatter.2.cloned.1.call-done = f32[128,1024]{1,0:T(8,128)} async-done(((f32[4096,1024]{1,0:T(8,128)}), f32[128,1024]{1,0:T(8,128)}) %reduce-scatter.2.cloned.1.call-update) | async-done | bytes 524304 | tf_op jit(solution)/shard_map/reduce_scatter | solution.py:102
  572.4 2.0 multiply_reduce_fusion
  574.4 44.3 %psum.7 = f32[]{:T(128)} all-reduce(f32[]{:T(128)} %get-tuple-element.93), channel_id=1, replica_groups=mesh['replica'=2,'fsdp'=16] {'replica','fsdp'}, use_global_device_ids=true, to_apply=%region_8.9 | all-reduce | flops 1 | bytes 8 | tf_op jit(solution)/shard_map/psum | solution.py:105
  619.4 4.7 all_gather.7
  624.2 1.1 slice_multiply_fusion
  (69 shorter events, 18.4 us)
Async XLA Ops:
  10.6 6.9 %copy-start.5 = (f32[256,512]{1,0:T(8,128)S(1)}, f32[256,512]{1,0:T(8,128)}, u32[]{:S(2)}) copy-start(f32[256,512]{1,0:T(8,128)} %param.15) | copy-start | bytes 1572868
  10.6 106.1 %all-to-all-start = ((bf16[16,256,512]{2,1,0:T(8,128)(2,1)}), bf16[16,256,512]{2,1,0:T(8,128)(2,1)}, u32[]{:S(2)}, u32[]{:S(2)}) async-start(bf16[16,256,512]{2,1,0:T(8,128)(2,1)} %stack.2), calls=%async_computation | async-start | bytes 8388608 | tf_op jit(solution)/shard_map/all_to_all | solution.py:60
  17.4 134.5 %all-gather.2.cloned.1.call-start = ((), (), s32[]{:S(2)}) async-start(), calls=%async_computation.2 | async-start | bytes 4456448 | tf_op jit(solution)/shard_map/all_gather | solution.py:69
  18.2 554.2 %reduce-scatter.2.cloned.1.call-start = ((), (), s32[]{:S(2)}) async-start(), calls=%async_computation.3 | async-start | bytes 17301504 | tf_op jit(solution)/shard_map/reduce_scatter | solution.py:102
  18.3 9.8 %copy-start.6 = (f32[4096]{0:T(1024)S(1)}, f32[4096]{0:T(1024)}, u32[]{:S(2)}) copy-start(f32[4096]{0:T(1024)} %param.13) | copy-start | bytes 49156
  24.8 3.4 copy-start.1
  29.3 1.9 copy-start.2
  122.9 35.6 %copy-start.9 = (s32[2]{0:T(128)S(1)}, s32[2]{0:T(128)}, u32[]{:S(2)}) copy-start(s32[2]{0:T(128)} %param.12) | copy-start | bytes 28
  158.5 4.2 copy-start.3
  173.4 2.2 copy-start
  176.5 1.1 copy-start.7
  176.5 2.7 copy-start.4
  178.4 0.8 copy-start.8
  179.2 4.2 copy-start.3
  194.1 2.2 copy-start
  197.2 1.1 copy-start.7
  197.2 2.7 copy-start.4
  199.1 0.8 copy-start.8
Sparse Core Ops, SparseCore 0:
  21.0 130.8 all-gather.1
  212.7 359.6 reduce-scatter.1
